TPU v7x, 32 devices: a whole 2x2x4 slice. The times are simulated.
32 devices in a mesh: depth: 4 (over z), imgx: 4 (over y, core), imgy: 2 (over x).
Axes of the slice: x: 2, y: 2, z: 4, core: 2. Of those that a mesh axis runs over, the one named last changes fastest.
Arguments:
- emissivity: bfloat16 [32, 512, 256], P('depth', 'imgx', 'imgy'), may hold values from 0.099609375 to 10
- bin_index: int32 [32, 512, 256], P('depth', 'imgx', 'imgy'), may hold values from 0 to 127
- color_table: bfloat16 [4, 128], replicated, may hold values from 0.049804688 to 1
- brick_order: int32 [4], replicated, may hold values from 0 to 3, each once
Outputs:
- image: float32 [4, 512, 256], P(None, 'imgx', 'imgy')
Inputs may be any that keep to these rules, and one draw needn't show every extreme that they name: brick_order names every brick index once.
All inputs are finite; a program needn't handle non-finite values.
Results may differ from a plain program's by a relative error of at most 0.0003.
Values sent between devices are 32-bit elements; how exact they have to be, the bound alone decides.
A program may use at most 64 MiB of HBM per device.

v0:
```python
import jax
import jax.numpy as jnp
from jax import lax
from jax.sharding import PartitionSpec as P


def on_device(emissivity, bin_index, color_table, brick_order):
    depth_cells, cols_x, cols_y = emissivity.shape
    pixels = cols_x * cols_y
    devices = lax.axis_size("depth")
    ray_step = 2.0 / (depth_cells * devices)
    levels = jnp.arange(color_table.shape[1], dtype=jnp.int32)

    def lookup(layer_bins):
        onehot = (layer_bins.reshape(1, pixels) == levels[:, None]).astype(jnp.bfloat16)
        return jnp.dot(color_table, onehot, preferred_element_type=jnp.float32)

    looked = lax.map(lookup, bin_index)
    bright = emissivity.reshape(depth_cells, pixels).astype(jnp.float32)
    glow_rgb = bright[:, None, :] * looked[:, 0:3, :]
    absorb_rate = bright * looked[:, 3, :]
    depth_in = jnp.cumsum(absorb_rate, axis=0) - absorb_rate
    light_in = jnp.exp(-ray_step * depth_in)
    color_sum = jnp.sum(ray_step * glow_rgb * light_in[:, None, :], axis=0)
    passed = jnp.exp(-ray_step * jnp.sum(absorb_rate, axis=0))
    piece_len = pixels // devices
    stacked = jnp.concatenate([color_sum, passed[None]], 0)[None]
    received = lax.all_to_all(stacked, "depth", split_axis=2, concat_axis=0, tiled=True)
    ordered = jnp.take(received, brick_order, axis=0)
    passed_all = ordered[:, 3, :]
    ahead_light = jnp.cumprod(
        jnp.concatenate([jnp.ones((1, piece_len), jnp.float32), passed_all[:-1]], 0), axis=0
    )
    my_color = jnp.sum(ordered[:, 0:3, :] * ahead_light[:, None, :], axis=0)
    through = jnp.prod(passed_all, axis=0)
    my_piece = jnp.concatenate([my_color, (1.0 - through)[None]], 0)
    full_tile = lax.all_gather(my_piece, "depth", axis=1, tiled=True)
    return full_tile.reshape(4, cols_x, cols_y)


def solution(mesh):
    return jax.shard_map(
        on_device,
        mesh=mesh,
        in_specs=(P("depth", "imgx", "imgy"), P("depth", "imgx", "imgy"), P(), P()),
        out_specs=P(None, "imgx", "imgy"),
        check_vma=False,
    )
```

profile of v0, /device:TPU:0, one launch (start us, length us, event | category | flops | bytes accessed | tf_op | source)
XLA Modules:
  0.0 172.7 jit_solution(10692280450666354)
XLA Ops:
  0.0 23.3 %while.11 = (s32[]{:T(128)}, f32[8,4,16384]{2,1,0:T(4,128)S(1)}, s32[8,128,128]{2,1,0:T(8,128)}, bf16[4,128]{1,0:T(4,128)(2,1)}, s32[]{:T(128)}) while((s32[]{:T(128)}, f32[8,4,16384]{2,1,0:T(4,128)S(1)}, s32[8,128,128]{2,1,0:T(8,128)}, bf16[4,128]{1,0:T(4,128)(2,1)}, s32[]{:T(128)}) %tuple.22), condition=%wide.region_1.2_spmd.clone, body=%wide.region_0.1_spmd.clone.sunk | while | flops 18874368 | bytes 459845 | solution.py:18
  0.0 0.9 dynamic-slice_bitcast_fusion.2
  0.9 2.1 %fusion.16 = f32[8,4,16384]{2,1,0:T(4,128)S(1)} fusion(f32[8,4,16384]{2,1,0:T(4,128)S(1)} %get-tuple-element.84, s32[]{:T(128)} %get-tuple-element.83, bf16[4,128]{1,0:T(4,128)(2,1)} %get-tuple-element.91, s32[16384]{0:T(1024)S(1)} %dynamic-slice_bitcast_fusion.2), kind=kOutput, calls=%fused_computation.3.clone.1 | convolution fusion | flops 18874368 | bytes 328708 | tf_op jit(solution)/shard_map/while/body/eval_jaxpr/dot_general | solution.py:16
  3.0 0.8 dynamic-slice_bitcast_fusion.2
  3.8 2.1 %fusion.16 = f32[8,4,16384]{2,1,0:T(4,128)S(1)} fusion(f32[8,4,16384]{2,1,0:T(4,128)S(1)} %get-tuple-element.84, s32[]{:T(128)} %get-tuple-element.83, bf16[4,128]{1,0:T(4,128)(2,1)} %get-tuple-element.91, s32[16384]{0:T(1024)S(1)} %dynamic-slice_bitcast_fusion.2), kind=kOutput, calls=%fused_computation.3.clone.1 | convolution fusion | flops 18874368 | bytes 328708 | tf_op jit(solution)/shard_map/while/body/eval_jaxpr/dot_general | solution.py:16
  6.7 2.1 %fusion.16 = f32[8,4,16384]{2,1,0:T(4,128)S(1)} fusion(f32[8,4,16384]{2,1,0:T(4,128)S(1)} %get-tuple-element.84, s32[]{:T(128)} %get-tuple-element.83, bf16[4,128]{1,0:T(4,128)(2,1)} %get-tuple-element.91, s32[16384]{0:T(1024)S(1)} %dynamic-slice_bitcast_fusion.2), kind=kOutput, calls=%fused_computation.3.clone.1 | convolution fusion | flops 18874368 | bytes 328708 | tf_op jit(solution)/shard_map/while/body/eval_jaxpr/dot_general | solution.py:16
  9.6 2.1 %fusion.16 = f32[8,4,16384]{2,1,0:T(4,128)S(1)} fusion(f32[8,4,16384]{2,1,0:T(4,128)S(1)} %get-tuple-element.84, s32[]{:T(128)} %get-tuple-element.83, bf16[4,128]{1,0:T(4,128)(2,1)} %get-tuple-element.91, s32[16384]{0:T(1024)S(1)} %dynamic-slice_bitcast_fusion.2), kind=kOutput, calls=%fused_computation.3.clone.1 | convolution fusion | flops 18874368 | bytes 328708 | tf_op jit(solution)/shard_map/while/body/eval_jaxpr/dot_general | solution.py:16
  12.5 2.1 %fusion.16 = f32[8,4,16384]{2,1,0:T(4,128)S(1)} fusion(f32[8,4,16384]{2,1,0:T(4,128)S(1)} %get-tuple-element.84, s32[]{:T(128)} %get-tuple-element.83, bf16[4,128]{1,0:T(4,128)(2,1)} %get-tuple-element.91, s32[16384]{0:T(1024)S(1)} %dynamic-slice_bitcast_fusion.2), kind=kOutput, calls=%fused_computation.3.clone.1 | convolution fusion | flops 18874368 | bytes 328708 | tf_op jit(solution)/shard_map/while/body/eval_jaxpr/dot_general | solution.py:16
  14.6 0.8 dynamic-slice_bitcast_fusion.2
  15.4 2.1 %fusion.16 = f32[8,4,16384]{2,1,0:T(4,128)S(1)} fusion(f32[8,4,16384]{2,1,0:T(4,128)S(1)} %get-tuple-element.84, s32[]{:T(128)} %get-tuple-element.83, bf16[4,128]{1,0:T(4,128)(2,1)} %get-tuple-element.91, s32[16384]{0:T(1024)S(1)} %dynamic-slice_bitcast_fusion.2), kind=kOutput, calls=%fused_computation.3.clone.1 | convolution fusion | flops 18874368 | bytes 328708 | tf_op jit(solution)/shard_map/while/body/eval_jaxpr/dot_general | solution.py:16
  18.3 2.1 %fusion.16 = f32[8,4,16384]{2,1,0:T(4,128)S(1)} fusion(f32[8,4,16384]{2,1,0:T(4,128)S(1)} %get-tuple-element.84, s32[]{:T(128)} %get-tuple-element.83, bf16[4,128]{1,0:T(4,128)(2,1)} %get-tuple-element.91, s32[16384]{0:T(1024)S(1)} %dynamic-slice_bitcast_fusion.2), kind=kOutput, calls=%fused_computation.3.clone.1 | convolution fusion | flops 18874368 | bytes 328708 | tf_op jit(solution)/shard_map/while/body/eval_jaxpr/dot_general | solution.py:16
  20.4 0.8 dynamic-slice_bitcast_fusion.2
  21.2 2.1 %fusion.16 = f32[8,4,16384]{2,1,0:T(4,128)S(1)} fusion(f32[8,4,16384]{2,1,0:T(4,128)S(1)} %get-tuple-element.84, s32[]{:T(128)} %get-tuple-element.83, bf16[4,128]{1,0:T(4,128)(2,1)} %get-tuple-element.91, s32[16384]{0:T(1024)S(1)} %dynamic-slice_bitcast_fusion.2), kind=kOutput, calls=%fused_computation.3.clone.1 | convolution fusion | flops 18874368 | bytes 328708 | tf_op jit(solution)/shard_map/while/body/eval_jaxpr/dot_general | solution.py:16
  23.9 1.2 fusion.6
  26.6 0.9 multiply_reduce_fusion
  27.6 5.1 %copy.8 = f32[4,16384]{0,1:T(8,128)} copy(f32[4,16384]{1,0:T(4,128)S(1)} %pad_maximum_fusion) | data formatting | bytes 524288 | tf_op jit(solution)/shard_map/concatenate | solution.py:27
  33.2 74.4 %reduce.1 = f32[16384,4]{1,0:T(8,128)} reduce(f32[16384,1,4]{2,1,0:T(1,128)} %bitcast.46, f32[]{:T(128)} %broadcast.39), dimensions={1}, to_apply=%bitcast.33.reduce_sub_computation | reduce | bytes 524292
  107.6 9.1 %reshape.72 = f32[4,1,16384]{2,1,0:T(1,128)} reshape(f32[16384,4]{1,0:T(8,128)} %reduce.1) | data formatting | bytes 524288
  116.7 6.3 %all-to-all-start = ((f32[4,1,16384]{2,1,0:T(1,128)}), f32[4,1,16384]{2,1,0:T(1,128)S(1)}, u32[]{:S(2)}, u32[]{:S(2)}) async-start(f32[4,1,16384]{2,1,0:T(1,128)} %reshape.72), calls=%async_computation | async-start | bytes 524288 | tf_op jit(solution)/shard_map/all_to_all | solution.py:28
  123.0 8.9 %all-to-all-done = f32[4,1,16384]{2,1,0:T(1,128)S(1)} async-done(((f32[4,1,16384]{2,1,0:T(1,128)}), f32[4,1,16384]{2,1,0:T(1,128)S(1)}, u32[]{:S(2)}, u32[]{:S(2)}) %all-to-all-start) | async-done | bytes 262176 | tf_op jit(solution)/shard_map/all_to_all | solution.py:28
  131.9 1.3 reduce.2
  133.2 17.7 %reshape.73 = f32[16384,1,4]{2,1,0:T(1,128)} reshape(f32[4,16384]{1,0:T(4,128)S(1)} %reduce.2) | data formatting | bytes 524288
  150.9 5.3 %copy.10 = f32[1,4,4,4096]{3,1,2,0:T(4,128)S(1)} copy(f32[1,4,4,4096]{1,3,2,0:T(8,128)} %bitcast.47) | data formatting | bytes 524288 | tf_op jit(solution)/shard_map/all_to_all | solution.py:28
  157.5 14.5 %all_gather.3 = f32[4,16384]{1,0:T(4,128)S(1)} all-gather(f32[4,4096]{1,0:T(4,128)S(1)} %pad_maximum_fusion.1), channel_id=1, replica_groups=mesh['depth'=4,'imgx'=4,'imgy'=2] {'depth'}, dimensions={1}, use_global_device_ids=true | all-gather | bytes 327680 | tf_op jit(solution)/shard_map/all_gather | solution.py:37
  (30 shorter events, 8.0 us)
Async XLA Ops:
  0.0 23.3 %copy-start = (bf16[8,128,128]{2,1,0:T(8,128)(2,1)S(1)}, bf16[8,128,128]{2,1,0:T(8,128)(2,1)}, u32[]{:S(2)}) copy-start(bf16[8,128,128]{2,1,0:T(8,128)(2,1)} %param.6) | copy-start | bytes 786436
  107.6 15.4 %copy-start.1 = (s32[4]{0:T(128)S(1)}, s32[4]{0:T(128)}, u32[]{:S(2)}) copy-start(s32[4]{0:T(128)} %param.9) | copy-start | bytes 52
  116.7 15.3 %all-to-all-start = ((f32[4,1,16384]{2,1,0:T(1,128)}), f32[4,1,16384]{2,1,0:T(1,128)S(1)}, u32[]{:S(2)}, u32[]{:S(2)}) async-start(f32[4,1,16384]{2,1,0:T(1,128)} %reshape.72), calls=%async_computation | async-start | bytes 524288 | tf_op jit(solution)/shard_map/all_to_all | solution.py:28
where the time goes:
time: 173 us
  other arithmetic  79.2 us (46%)
  local copies, waits for them, and re-layouts  47.1 us (27%)
  matrix products  16.5 us (10%)
  blocking collectives  14.5 us (8%)
  waiting for transfers between devices  8.87 us (5%)
  starting transfers between devices  6.35 us (4%)
    unnamed x1, other arithmetic  74.4 us
    unnamed x11, local copies, waits for them, and re-layouts  28.7 us
    dot_general x8, matrix products, lookup(): return jnp.dot(color_table, onehot, preferred_element_type=jnp.float32)  16.5 us
    all_gather x1, blocking collectives, on_device(): full_tile = lax.all_gather(my_piece, 'depth', axis=1, tiled=True)  14.5 us
    all_to_all x1, waiting for transfers between devices, on_device(): lax.all_to_all(stacked, 'depth', split_axis=2, concat_axis=0, tiled=True)  8.87 us
    eq x8, local copies, waits for them, and re-layouts, lookup(): layer_bins.reshape(1, pixels) == levels[:, None]  6.79 us
    all_to_all x1, starting transfers between devices, on_device(): lax.all_to_all(stacked, 'depth', split_axis=2, concat_axis=0, tiled=True)  6.35 us
    all_to_all x1, local copies, waits for them, and re-layouts, on_device(): lax.all_to_all(stacked, 'depth', split_axis=2, concat_axis=0, tiled=True)  5.3 us
  transfers between devices with their start and end apart: 1, of which 1 were waited for; matrix products, arithmetic and copies ran while one was open for 0% of the time, Pallas kernels for 0%

commit v1 on v0

v1 whole, which is shorter than its diff:
```python
import functools

import jax
import jax.numpy as jnp
from jax import lax
from jax.experimental import pallas as pl
from jax.experimental.pallas import tpu as pltpu
from jax.sharding import PartitionSpec as P

MESH = pl.DeviceIdType.MESH
BLOCK = 16
LANES = 128


def look(channel_tables, bins):
    slabs = len(channel_tables[0])
    if slabs == 1:
        return [jnp.take_along_axis(t[0], bins, axis=1, mode="promise_in_bounds") for t in channel_tables]
    within = bins % LANES
    slab_of = bins // LANES
    out = []
    for t in channel_tables:
        value = jnp.take_along_axis(t[0], within, axis=1, mode="promise_in_bounds")
        for s in range(1, slabs):
            other = jnp.take_along_axis(t[s], within, axis=1, mode="promise_in_bounds")
            value = jnp.where(slab_of == s, other, value)
        out.append(value)
    return out


def scaled_tables(table_ref, ray_step):
    table = table_ref[...].astype(jnp.float32) * ray_step
    slabs = table.shape[1] // LANES
    return [
        [jnp.broadcast_to(table[c : c + 1, s * LANES : (s + 1) * LANES], (BLOCK, LANES)) for s in range(slabs)]
        for c in range(4)
    ]


def march(tables, emis_ref, bins_ref, start):
    cells = emis_ref.shape[0]
    rows = pl.ds(start, BLOCK)
    color = [None] * 3
    depth_in = None
    for z in range(cells):
        bright = emis_ref[z, rows, :].astype(jnp.float32)
        looked = look(tables, bins_ref[z, rows, :])
        rate = bright * looked[3]
        if depth_in is None:
            color = [bright * looked[c] for c in range(3)]
            depth_in = rate
        else:
            seen = bright * jnp.exp(-depth_in)
            color = [color[c] + seen * looked[c] for c in range(3)]
            depth_in = depth_in + rate
    return color + [jnp.exp(-depth_in)]


def fused(n, ray_step, emis_hbm, bins_hbm, table_ref, order_ref, out_ref,
          emis, bins, outgoing, arrived, mine, in_sem, send_sem, recv_sem, give_sem, take_sem):
    me = lax.axis_index("depth")
    rows = mine.shape[1]
    hops = sorted(range(1, n), key=lambda h: (-min(h, n - h), h)) + [0]

    def at_hop(h):
        return lax.rem(me + h, n)

    def span(d):
        return pl.ds(pl.multiple_of(d * rows, BLOCK), rows)

    loads = []
    for i, h in enumerate(hops):
        dest = span(at_hop(h))
        pair = (
            pltpu.make_async_copy(emis_hbm.at[:, dest, :], emis.at[i], in_sem.at[2 * i]),
            pltpu.make_async_copy(bins_hbm.at[:, dest, :], bins.at[i], in_sem.at[2 * i + 1]),
        )
        for c in pair:
            c.start()
        loads.append(pair)

    barrier = pltpu.get_barrier_semaphore()
    for h in range(1, n):
        pl.semaphore_signal(barrier, inc=1, device_id={"depth": at_hop(h)}, device_id_type=MESH)

    tables = scaled_tables(table_ref, ray_step)
    sends = []
    for i, h in enumerate(hops):
        for c in loads[i]:
            c.wait()
        for r in range(0, rows, BLOCK):
            part = march(tables, emis.at[i], bins.at[i], r)
            for c in range(4):
                if h == 0:
                    arrived[me, c, pl.ds(r, BLOCK), :] = part[c]
                else:
                    outgoing[i, c, pl.ds(r, BLOCK), :] = part[c]
        if h != 0:
            if i == 0:
                pl.semaphore_wait(barrier, n - 1)
            copy = pltpu.make_async_remote_copy(
                src_ref=outgoing.at[i],
                dst_ref=arrived.at[me],
                send_sem=send_sem.at[i],
                recv_sem=recv_sem.at[i],
                device_id={"depth": at_hop(h)},
                device_id_type=MESH,
            )
            copy.start()
            sends.append(copy)
    for copy in sends:
        copy.wait_recv()

    for r in range(0, rows, BLOCK):
        at = pl.ds(r, BLOCK)
        first = order_ref[0]
        color = [arrived[first, c, at, :] for c in range(3)]
        through = arrived[first, 3, at, :]
        for k in range(1, n):
            b = order_ref[k]
            color = [color[c] + through * arrived[b, c, at, :] for c in range(3)]
            through = through * arrived[b, 3, at, :]
        for c in range(3):
            mine[c, at, :] = color[c]
        mine[3, at, :] = 1.0 - through

    gives = []
    for i, h in enumerate(hops[:-1]):
        copy = pltpu.make_async_remote_copy(
            src_ref=mine,
            dst_ref=out_ref.at[:, span(me), :],
            send_sem=give_sem.at[i],
            recv_sem=take_sem.at[i],
            device_id={"depth": at_hop(h)},
            device_id_type=MESH,
        )
        copy.start()
        gives.append(copy)
    out_ref[:, span(me), :] = mine[...]
    for copy in sends:
        copy.wait_send()
    for copy in gives:
        copy.wait()


def fused_call(emissivity, bin_index, color_table, brick_order, n, ray_step):
    cells, cols_x, cols_y = emissivity.shape
    rows = cols_x // n
    return pl.pallas_call(
        functools.partial(fused, n, ray_step),
        out_shape=jax.ShapeDtypeStruct((4, cols_x, cols_y), jnp.float32),
        in_specs=[
            pl.BlockSpec(memory_space=pltpu.HBM),
            pl.BlockSpec(memory_space=pltpu.HBM),
            pl.BlockSpec(memory_space=pltpu.VMEM),
            pl.BlockSpec(memory_space=pltpu.SMEM),
        ],
        out_specs=pl.BlockSpec(memory_space=pltpu.VMEM),
        scratch_shapes=[
            pltpu.VMEM((n, cells, rows, cols_y), jnp.bfloat16),
            pltpu.VMEM((n, cells, rows, cols_y), jnp.int32),
            pltpu.VMEM((n - 1, 4, rows, cols_y), jnp.float32),
            pltpu.VMEM((n, 4, rows, cols_y), jnp.float32),
            pltpu.VMEM((4, rows, cols_y), jnp.float32),
            pltpu.SemaphoreType.DMA((2 * n,)),
            pltpu.SemaphoreType.DMA((n - 1,)),
            pltpu.SemaphoreType.DMA((n - 1,)),
            pltpu.SemaphoreType.DMA((n - 1,)),
            pltpu.SemaphoreType.DMA((n - 1,)),
        ],
        compiler_params=pltpu.CompilerParams(collective_id=0, has_side_effects=True),
    )(emissivity, bin_index, color_table, brick_order)


def march_kernel(ray_step, emis_ref, bins_ref, table_ref, out_ref):
    tables = scaled_tables(table_ref, ray_step)

    @pl.loop(0, emis_ref.shape[1] // BLOCK)
    def _(r):
        start = pl.multiple_of(r * BLOCK, BLOCK)
        part = march(tables, emis_ref, bins_ref, start)
        for c in range(4):
            out_ref[c, pl.ds(start, BLOCK), :] = part[c]


def spread(emissivity, bin_index, color_table, brick_order, n, ray_step):
    cells, cols_x, cols_y = emissivity.shape
    piece_len = cols_x * cols_y // n
    stacked = pl.pallas_call(
        functools.partial(march_kernel, ray_step),
        out_shape=jax.ShapeDtypeStruct((4, cols_x, cols_y), jnp.float32),
        in_specs=[pl.BlockSpec(memory_space=pltpu.VMEM)] * 3,
        out_specs=pl.BlockSpec(memory_space=pltpu.VMEM),
    )(emissivity, bin_index, color_table)
    stacked = stacked.reshape(1, 4, n, piece_len).transpose(2, 0, 1, 3).reshape(n, 4, piece_len)
    received = lax.all_to_all(stacked, "depth", split_axis=0, concat_axis=0, tiled=True)
    ordered = jnp.take(received, brick_order, axis=0)
    color, through = ordered[0, 0:3], ordered[0, 3]
    for k in range(1, n):
        color = color + through * ordered[k, 0:3]
        through = through * ordered[k, 3]
    piece = jnp.concatenate([color, (1.0 - through)[None]], 0)
    return lax.all_gather(piece, "depth", axis=1, tiled=True).reshape(4, cols_x, cols_y)


def on_device(emissivity, bin_index, color_table, brick_order):
    cells, cols_x, cols_y = emissivity.shape
    n = lax.axis_size("depth")
    ray_step = 2.0 / (cells * n)
    piecewise = cols_x % (n * BLOCK) == 0
    form = fused_call if piecewise else spread
    return form(emissivity, bin_index, color_table, brick_order, n, ray_step)


def solution(mesh):
    return jax.shard_map(
        on_device,
        mesh=mesh,
        in_specs=(P("depth", "imgx", "imgy"), P("depth", "imgx", "imgy"), P(), P()),
        out_specs=P(None, "imgx", "imgy"),
        check_vma=False,
    )
```

time: 173 us -> 20.9 us (0.12)
  other arithmetic: 79.2 us -> 0 us
  local copies, waits for them, and re-layouts: 47.1 us -> 1.67 us
  Pallas kernels: 0 us -> 19 us
  matrix products: 16.5 us -> 0 us
  blocking collectives: 14.5 us -> 0 us
  waiting for transfers between devices: 8.87 us -> 0 us
  starting transfers between devices: 6.35 us -> 0 us
    unnamed x1 -> x0, other arithmetic: 74.4 us -> none
    unnamed x11 -> x1, local copies, waits for them, and re-layouts: 28.7 us -> 1.67 us
    pallas_call x0 -> x1, Pallas kernels: none -> 19 us  [fused_call(): pl.pallas_call(functools.partial(fused, n, ray_step), out_shape=jax.Shape...]
    dot_general x8 -> x0, matrix products: 16.5 us -> none  [lookup(): return jnp.dot(color_table, onehot, preferred_element_type=jnp.float32)]
    all_gather x1 -> x0, blocking collectives: 14.5 us -> none  [on_device(): full_tile = lax.all_gather(my_piece, 'depth', axis=1, tiled=True)]
    all_to_all x1 -> x0, waiting for transfers between devices: 8.87 us -> none  [on_device(): lax.all_to_all(stacked, 'depth', split_axis=2, concat_axis=0, tiled=True)]
    eq x8 -> x0, local copies, waits for them, and re-layouts: 6.79 us -> none  [lookup(): layer_bins.reshape(1, pixels) == levels[:, None]]
    all_to_all x1 -> x0, starting transfers between devices: 6.35 us -> none  [on_device(): lax.all_to_all(stacked, 'depth', split_axis=2, concat_axis=0, tiled=True)]
  transfers between devices with their start and end apart: 1 -> 0, of which waited for: 1 -> 0; matrix products, arithmetic and copies ran while one was open for 0% -> 0% of each run, Pallas kernels for 0% -> 0%
where the time goes in v1:
time: 20.9 us; the launch traced here: 20.7 us
  Pallas kernels  19 us (91%)
  local copies, waits for them, and re-layouts  1.67 us (8%)
    pallas_call x1, Pallas kernels, fused_call(): pl.pallas_call(functools.partial(fused, n, ray_step), out_shape=jax.Shape...  19 us
    unnamed x1, local copies, waits for them, and re-layouts  1.67 us

profile of v1, /device:TPU:0, one launch (start us, length us, event | category | flops | bytes accessed | tf_op | source)
XLA Modules:
  0.0 20.7 jit_solution(12193817545032869773)
XLA Ops:
  0.0 19.0 %shard_map.46 = f32[4,128,128]{2,1,0:T(8,128)} custom-call(bf16[8,128,128]{2,1,0:T(8,128)(2,1)} %emis_hbm.1, s32[8,128,128]{2,1,0:T(8,128)} %bins_hbm.1, bf16[4,128]{1,0:T(4,128)(2,1)} %table_ref.1, s32[4]{0:T(128)} %order_ref.1), custom_call_target="tpu_custom_call" | custom-call | tf_op jit(solution)/shard_map/pallas_call | solution.py:149
  19.0 1.7 %copy.6 = f32[4,128,128]{2,1,0:T(8,128)} copy(f32[4,128,128]{2,1,0:T(8,128)} %shard_map.46) | data formatting | bytes 524288

commit v2 on v1

--- a/solution.py
+++ b/solution.py
@@ -148,7 +148,7 @@
     rows = cols_x // n
     return pl.pallas_call(
         functools.partial(fused, n, ray_step),
-        out_shape=jax.ShapeDtypeStruct((4, cols_x, cols_y), jnp.float32),
+        out_shape=pltpu.VMEM((4, cols_x, cols_y), jnp.float32),
         in_specs=[
             pl.BlockSpec(memory_space=pltpu.HBM),
             pl.BlockSpec(memory_space=pltpu.HBM),

time: 20.9 us -> 19.2 us (0.919)
  local copies, waits for them, and re-layouts: 1.67 us -> 0.71 us
  Pallas kernels: 19 us -> 18.3 us
    unnamed x1, local copies, waits for them, and re-layouts: 1.67 us -> 0.71 us
    pallas_call x1, Pallas kernels: 19 us -> 18.3 us  [fused_call(): pl.pallas_call(functools.partial(fused, n, ray_step), out_shape=pltpu.VME...]
where the time goes in v2:
time: 19.2 us; the launch traced here: 19.1 us
  Pallas kernels  18.3 us (95%)
  local copies, waits for them, and re-layouts  0.71 us (4%)
    pallas_call x1, Pallas kernels, fused_call(): pl.pallas_call(functools.partial(fused, n, ray_step), out_shape=pltpu.VME...  18.3 us
    unnamed x1, local copies, waits for them, and re-layouts  0.71 us

profile of v2, /device:TPU:0, one launch (start us, length us, event | category | flops | bytes accessed | tf_op | source)
XLA Modules:
  0.0 19.1 jit_solution(7035542136006978645)
XLA Ops:
  0.0 18.3 %shard_map.46 = f32[4,128,128]{2,1,0:T(8,128)S(1)} custom-call(bf16[8,128,128]{2,1,0:T(8,128)(2,1)} %emis_hbm.1, s32[8,128,128]{2,1,0:T(8,128)} %bins_hbm.1, bf16[4,128]{1,0:T(4,128)(2,1)} %table_ref.1, s32[4]{0:T(128)} %order_ref.1), custom_call_target="tpu_custom_call" | custom-call | tf_op jit(solution)/shard_map/pallas_call | solution.py:149
  18.4 0.7 %copy.6 = f32[4,128,128]{2,1,0:T(8,128)} copy(f32[4,128,128]{2,1,0:T(8,128)S(1)} %shard_map.46) | data formatting | bytes 524288

commit v3 on v2

--- a/solution.py
+++ b/solution.py
@@ -60,7 +60,7 @@
           emis, bins, outgoing, arrived, mine, in_sem, send_sem, recv_sem, give_sem, take_sem):
     me = lax.axis_index("depth")
     rows = mine.shape[1]
-    hops = sorted(range(1, n), key=lambda h: (-min(h, n - h), h)) + [0]
+    hops = sorted(range(1, n), key=lambda h: min(h, n - h)) + [0]
 
     def at_hop(h):
         return lax.rem(me + h, n)

time: 19.2 us -> 18.8 us (0.979)
  Pallas kernels: 18.3 us -> 18 us
    pallas_call x1, Pallas kernels: 18.3 us -> 18 us  [fused_call(): pl.pallas_call(functools.partial(fused, n, ray_step), out_shape=pltpu.VME...]
where the time goes in v3:
time: 18.8 us; the launch traced here: 18.7 us
  Pallas kernels  18 us (96%)
  local copies, waits for them, and re-layouts  0.71 us (4%)
    pallas_call x1, Pallas kernels, fused_call(): pl.pallas_call(functools.partial(fused, n, ray_step), out_shape=pltpu.VME...  18 us
    unnamed x1, local copies, waits for them, and re-layouts  0.71 us

profile of v3, /device:TPU:0, one launch (start us, length us, event | category | flops | bytes accessed | tf_op | source)
XLA Modules:
  0.0 18.7 jit_solution(5153895780417804144)
XLA Ops:
  0.0 18.0 %shard_map.46 = f32[4,128,128]{2,1,0:T(8,128)S(1)} custom-call(bf16[8,128,128]{2,1,0:T(8,128)(2,1)} %emis_hbm.1, s32[8,128,128]{2,1,0:T(8,128)} %bins_hbm.1, bf16[4,128]{1,0:T(4,128)(2,1)} %table_ref.1, s32[4]{0:T(128)} %order_ref.1), custom_call_target="tpu_custom_call" | custom-call | tf_op jit(solution)/shard_map/pallas_call | solution.py:149
  18.0 0.7 %copy.6 = f32[4,128,128]{2,1,0:T(8,128)} copy(f32[4,128,128]{2,1,0:T(8,128)S(1)} %shard_map.46) | data formatting | bytes 524288
